TPU v7x, 32 devices: a whole 2x2x4 slice. The times are simulated.
32 devices in a mesh: section: 4 (over y, core), tensor: 8 (over z, x).
Axes of the slice: x: 2, y: 2, z: 4, core: 2. Of those that a mesh axis runs over, the one named last changes fastest.
Arguments:
- saved_inputs: bfloat16 [4, 4, 256, 1024], P('section', None, 'tensor'), may hold values from -6 to 6
- slot_index: int32 [4, 3], P('section'), may hold values from 0 to 3
- example_lengths: int32 [4, 3, 2], P('section'), may hold values from 1 to 192, 256 in all within a row
- first_grads: bfloat16 [4, 256, 1024], P('section', 'tensor'), may hold values from -6 to 6
- loss_grads: bfloat16 [2, 256, 1024], P(None, 'tensor'), may hold values from -6 to 6
- w_in: bfloat16 [4, 1024, 32768], P('section', None, 'tensor'), may hold values from -0.1875 to 0.1875
- w_out: bfloat16 [4, 32768, 1024], P('section', 'tensor'), may hold values from -0.03125 to 0.03125
Outputs:
- grad_in: bfloat16 [4, 1024, 32768], P('section', None, 'tensor')
- grad_out: bfloat16 [4, 32768, 1024], P('section', 'tensor')
- input_grads: bfloat16 [4, 3, 256, 1024], P('section', None, 'tensor')
Inputs may be any that keep to these rules, and one draw needn't show every extreme that they name: `example_lengths`: the 2 lengths of one microbatch sum to 256.
All inputs are finite; a program needn't handle non-finite values.
Results may differ from a plain program's by a relative error of at most 0.0095.
Values may be sent and summed in bfloat16 or wider, within the bound.
A program may use at most 128 MiB of HBM per device.

v0:
```python
import jax
import jax.numpy as jnp
from jax import lax
from jax.sharding import PartitionSpec as P

D = 1024
FF = 32768
GAMMA = 0.01


def shifted(value, axis, steps):
    count = lax.axis_size(axis)
    first, last = (max(0, -steps), min(count, count - steps))
    return lax.ppermute(value, axis, [(source, source + steps) for source in range(first, last)])


def membership(lengths, tokens):
    ends = jnp.cumsum(lengths)
    position = jnp.arange(tokens, dtype=jnp.int32)
    example_id = jnp.sum((position[:, None] >= ends[None, :-1]).astype(jnp.int32), axis=1)
    labels = jnp.arange(lengths.shape[0], dtype=jnp.int32)
    return (example_id[:, None] == labels[None, :]).astype(jnp.float32)


def per_device(saved_inputs, slot_index, example_lengths, first_grads, loss_grads, w_in, w_out):
    section_count = lax.axis_size("section")
    is_last = lax.axis_index("section") == section_count - 1
    first = w_in[0]
    second = w_out[0]
    slot_count = loss_grads.shape[0] + 1
    rows = first_grads.shape[1]
    picked = [
        lax.dynamic_index_in_dim(saved_inputs[0], slot_index[0, slot], 0, keepdims=False)
        for slot in range(slot_count)
    ]
    every_input = lax.all_gather(jnp.stack(picked), "tensor", axis=1, tiled=True)
    acc_first = jnp.zeros(first.shape, jnp.float32)
    acc_second = jnp.zeros(second.shape, jnp.float32)
    incoming = first_grads[0]
    results = []
    for slot in range(slot_count):
        inputs = every_input[slot]
        grads = lax.all_gather(incoming, "tensor", axis=0, tiled=True)
        z = jnp.dot(inputs, first, preferred_element_type=jnp.float32)
        relu = jnp.maximum(z, 0.0)
        hidden = (relu * relu).astype(jnp.bfloat16)
        back = jnp.einsum("td,fd->tf", grads, second, preferred_element_type=jnp.float32)
        dz = (2.0 * relu * back).astype(jnp.bfloat16)
        own_terms = jnp.einsum("tf,df->td", dz, first, preferred_element_type=jnp.float32)
        summed = lax.psum(own_terms, "tensor")
        shares = lax.dynamic_slice_in_dim(summed, lax.axis_index("tensor") * rows, rows, 0)
        member = membership(example_lengths[0, slot], inputs.shape[0])
        pieces = []
        for example in range(member.shape[1]):
            keep = member[:, example][:, None].astype(jnp.bfloat16)
            per_first = jnp.einsum(
                "td,tf->df", inputs * keep, dz, preferred_element_type=jnp.float32
            )
            per_second = jnp.einsum(
                "tf,td->fd", hidden, grads * keep, preferred_element_type=jnp.float32
            )
            pieces.append(jnp.sum(per_first * per_first) + jnp.sum(per_second * per_second))
        local_squares = jnp.stack(pieces)
        squares = lax.psum(local_squares, "tensor")
        factor = 1.0 / (jnp.sqrt(squares / (D * FF)) + GAMMA)
        token_factor = jnp.sum(member * factor[None, :], axis=1)
        dzc = (dz.astype(jnp.float32) * token_factor[:, None]).astype(jnp.bfloat16)
        dyc = (grads.astype(jnp.float32) * token_factor[:, None]).astype(jnp.bfloat16)
        acc_first = acc_first + jnp.einsum(
            "td,tf->df", inputs, dzc, preferred_element_type=jnp.float32
        )
        acc_second = acc_second + jnp.einsum(
            "tf,td->fd", hidden, dyc, preferred_element_type=jnp.float32
        )
        passing = (incoming.astype(jnp.float32) + shares).astype(jnp.bfloat16)
        results.append(passing)
        if slot + 1 < slot_count:
            arrived = shifted(passing, "section", -1)
            incoming = jnp.where(is_last, loss_grads[slot], arrived)
    grad_in = acc_first.astype(jnp.bfloat16)[None]
    grad_out = acc_second.astype(jnp.bfloat16)[None]
    input_grads = jnp.stack(results)[None]
    return (grad_in, grad_out, input_grads)


def solution(mesh):
    return jax.shard_map(
        per_device,
        mesh=mesh,
        in_specs=(
            P("section", None, "tensor", None),
            P("section", None),
            P("section", None, None),
            P("section", "tensor", None),
            P(None, "tensor", None),
            P("section", None, "tensor"),
            P("section", "tensor", None),
        ),
        out_specs=(
            P("section", None, "tensor"),
            P("section", "tensor", None),
            P("section", None, "tensor", None),
        ),
        check_vma=False,
    )
```

profile of v0, /device:TPU:0, one launch (start us, length us, event | category | flops | bytes accessed | tf_op | source)
XLA Modules:
  0.0 492.9 jit_solution(11279649531270042013)
XLA Ops:
  7.2 1.4 fusion.83
  14.4 0.9 dynamic-slice_bitcast_fusion.2
  15.3 0.7 pad_maximum_fusion
  16.1 1.0 slice_reduce_fusion.6
  17.9 34.0 %all-gather = bf16[1,256,1024]{2,1,0:T(8,128)(2,1)S(1)} all-gather(bf16[1,32,1024]{2,1,0:T(8,128)(2,1)} %param.10), channel_id=2, replica_groups=mesh['section'=4,'tensor'=8] {'tensor'}, dimensions={1}, use_global_device_ids=true | all-gather | bytes 589824 | tf_op jit(solution)/shard_map/all_gather | solution.py:43
  51.9 12.3 %all-gather.3.cloned.1.call-done = bf16[3,256,1024]{2,1,0:T(8,128)(2,1)} async-done(((bf16[3,32,1024]{2,1,0:T(8,128)(2,1)}), bf16[3,256,1024]{2,1,0:T(8,128)(2,1)}) %all-gather.3.cloned.1.call-update) | async-done | bytes 1572880 | tf_op jit(solution)/shard_map/all_gather | solution.py:36
  64.2 5.9 %fusion.20 = f32[256,4096]{1,0:T(8,128)S(1)} fusion(bf16[1,1024,4096]{2,1,0:T(8,128)(2,1)} %param.12, bf16[3,256,1024]{2,1,0:T(8,128)(2,1)} %all-gather.3.cloned.1.call-done), kind=kOutput, calls=%fused_computation.34 | convolution fusion | flops 2148532224 | bytes 13107200 | tf_op jit(solution)/shard_map/dot_general | solution.py:44
  70.2 5.2 %multiply_reduce_fusion.8 = f32[]{:T(128)} fusion(bf16[1,256,1024]{2,1,0:T(8,128)(2,1)S(1)} %all-gather, bf16[256]{0:T(256)(128)(2,1)S(1)} %get-tuple-element.11, f32[256,4096]{1,0:T(8,128)S(1)} %fusion.20), kind=kOutput, calls=%fused_computation.10 | convolution fusion | flops 2158231552 | bytes 4719108 | tf_op jit(solution)/shard_map/tf,td->fd/dot_general | solution.py:59
  75.4 5.2 %multiply_reduce_fusion.10 = f32[]{:T(128)} fusion(bf16[1,256,1024]{2,1,0:T(8,128)(2,1)S(1)} %all-gather, bf16[256]{0:T(256)(128)(2,1)S(1)} %get-tuple-element.10, f32[256,4096]{1,0:T(8,128)S(1)} %fusion.20), kind=kOutput, calls=%fused_computation.12 | convolution fusion | flops 2158231552 | bytes 4719108 | tf_op jit(solution)/shard_map/tf,td->fd/dot_general | solution.py:59
  80.6 13.6 %fusion.44 = bf16[256,4096]{1,0:T(8,128)(2,1)S(1)} fusion(bf16[1,4096,1024]{2,1,0:T(8,128)(2,1)S(1)} %bitcast.137, f32[256,4096]{1,0:T(8,128)S(1)} %fusion.20, bf16[1,256,1024]{2,1,0:T(8,128)(2,1)S(1)} %all-gather), kind=kOutput, calls=%fused_computation.42 | convolution fusion | flops 2150629376 | bytes 15204352 | tf_op jit(solution)/shard_map/td,fd->tf/dot_general | solution.py:47
  94.2 7.5 %fusion.12 = f32[256,1024]{1,0:T(8,128)} fusion(bf16[256,4096]{1,0:T(8,128)(2,1)S(1)} %fusion.44, bf16[1,1024,4096]{2,1,0:T(8,128)(2,1)} %param.12), kind=kOutput, calls=%fused_computation.26 | convolution fusion | flops 2147483648 | bytes 11534336 | tf_op jit(solution)/shard_map/tf,df->td/dot_general | solution.py:49
  101.8 6.3 %multiply_reduce_fusion.9 = f32[]{:T(128)} fusion(bf16[256,4096]{1,0:T(8,128)(2,1)S(1)} %fusion.44, bf16[3,256,1024]{2,1,0:T(8,128)(2,1)} %all-gather.3.cloned.1.call-done, bf16[256]{0:T(256)(128)(2,1)S(1)} %get-tuple-element.11), kind=kOutput, calls=%fused_computation.11 | convolution fusion | flops 2156134400 | bytes 2621956 | tf_op jit(solution)/shard_map/td,tf->df/dot_general | solution.py:56
  109.4 6.3 %multiply_reduce_fusion.11 = f32[]{:T(128)} fusion(bf16[256,4096]{1,0:T(8,128)(2,1)S(1)} %fusion.44, bf16[3,256,1024]{2,1,0:T(8,128)(2,1)} %all-gather.3.cloned.1.call-done, bf16[256]{0:T(256)(128)(2,1)S(1)} %get-tuple-element.10), kind=kOutput, calls=%fused_computation.13 | convolution fusion | flops 2156134400 | bytes 2621956 | tf_op jit(solution)/shard_map/td,tf->df/dot_general | solution.py:56
  117.0 8.0 %fusion.26 = f32[256,4096]{1,0:T(8,128)} fusion(bf16[1,1024,4096]{2,1,0:T(8,128)(2,1)} %param.12, bf16[3,256,1024]{2,1,0:T(8,128)(2,1)} %all-gather.3.cloned.1.call-done), kind=kOutput, calls=%fused_computation.36 | convolution fusion | flops 2148532224 | bytes 13107200 | tf_op jit(solution)/shard_map/dot_general | solution.py:44
  125.0 8.5 %fusion.23 = f32[256,4096]{1,0:T(8,128)} fusion(bf16[1,1024,4096]{2,1,0:T(8,128)(2,1)} %param.12, bf16[3,256,1024]{2,1,0:T(8,128)(2,1)} %all-gather.3.cloned.1.call-done), kind=kOutput, calls=%fused_computation.35 | convolution fusion | flops 2148532224 | bytes 13107200 | tf_op jit(solution)/shard_map/dot_general | solution.py:44
  133.5 45.7 %all-reduce.5.cloned.1.call-done = f32[256,1024]{1,0:T(8,128)} async-done(((f32[256,1024]{1,0:T(8,128)}), f32[256,1024]{1,0:T(8,128)}) %all-reduce.5.cloned.1.call-update) | async-done | bytes 1048592 | tf_op jit(solution)/shard_map/psum | solution.py:50
  179.2 0.9 fusion.81
  180.1 1.3 collective-permute-start
  181.5 1.8 collective-permute-done
  183.2 31.3 %all_gather.14 = bf16[256,1024]{1,0:T(8,128)(2,1)S(1)} all-gather(bf16[32,1024]{1,0:T(8,128)(2,1)S(1)} %bitcast_select_fusion.1), channel_id=1, replica_groups=mesh['section'=4,'tensor'=8] {'tensor'}, dimensions={0}, use_global_device_ids=true | all-gather | bytes 589824 | tf_op jit(solution)/shard_map/all_gather | solution.py:43
  214.5 7.2 %fusion.41 = bf16[256,4096]{1,0:T(8,128)(2,1)S(1)} fusion(bf16[256,1024]{1,0:T(8,128)(2,1)S(1)} %all_gather.14, bf16[1,4096,1024]{2,1,0:T(8,128)(2,1)} %param.13, f32[256,4096]{1,0:T(8,128)} %fusion.23), kind=kOutput, calls=%fused_computation.41 | convolution fusion | flops 2150629376 | bytes 15204352 | tf_op jit(solution)/shard_map/td,fd->tf/dot_general | solution.py:47
  221.8 5.2 %multiply_reduce_fusion.4 = f32[]{:T(128)} fusion(bf16[256,1024]{1,0:T(8,128)(2,1)S(1)} %all_gather.14, bf16[256]{0:T(256)(128)(2,1)S(1)} %get-tuple-element.9, f32[256,4096]{1,0:T(8,128)S(1)} %copy-done.2), kind=kOutput, calls=%fused_computation.6 | convolution fusion | flops 2158231552 | bytes 4719108 | tf_op jit(solution)/shard_map/tf,td->fd/dot_general | solution.py:59
  226.9 6.8 %fusion.8 = f32[256,1024]{1,0:T(8,128)} fusion(bf16[256,4096]{1,0:T(8,128)(2,1)S(1)} %fusion.41, bf16[1,1024,4096]{2,1,0:T(8,128)(2,1)} %param.12), kind=kOutput, calls=%fused_computation.22 | convolution fusion | flops 2147483648 | bytes 11534336 | tf_op jit(solution)/shard_map/tf,df->td/dot_general | solution.py:49
  233.7 0.2 all-reduce.9.cloned.1.call-start
  234.0 6.3 %multiply_reduce_fusion.5 = f32[]{:T(128)} fusion(bf16[256,4096]{1,0:T(8,128)(2,1)S(1)} %fusion.41, bf16[3,256,1024]{2,1,0:T(8,128)(2,1)} %all-gather.3.cloned.1.call-done, bf16[256]{0:T(256)(128)(2,1)S(1)} %get-tuple-element.9), kind=kOutput, calls=%fused_computation.7 | convolution fusion | flops 2156134400 | bytes 2621956 | tf_op jit(solution)/shard_map/td,tf->df/dot_general | solution.py:56
  241.5 6.5 %multiply_reduce_fusion.7 = f32[]{:T(128)} fusion(bf16[256,4096]{1,0:T(8,128)(2,1)S(1)} %fusion.41, bf16[3,256,1024]{2,1,0:T(8,128)(2,1)} %all-gather.3.cloned.1.call-done, bf16[256]{0:T(256)(128)(2,1)S(1)} %get-tuple-element.8), kind=kOutput, calls=%fused_computation.9 | convolution fusion | flops 2156134400 | bytes 2621956 | tf_op jit(solution)/shard_map/td,tf->df/dot_general | solution.py:56
  248.0 5.6 %multiply_reduce_fusion.6 = f32[]{:T(128)} fusion(bf16[256,1024]{1,0:T(8,128)(2,1)S(1)} %all_gather.14, bf16[256]{0:T(256)(128)(2,1)S(1)} %get-tuple-element.8, f32[256,4096]{1,0:T(8,128)S(1)} %copy-done.3), kind=kOutput, calls=%fused_computation.8 | convolution fusion | flops 2158231552 | bytes 4719108 | tf_op jit(solution)/shard_map/tf,td->fd/dot_general | solution.py:59
  254.9 57.6 %all-reduce.7.cloned.1.call-done = f32[256,1024]{1,0:T(8,128)} async-done(((f32[256,1024]{1,0:T(8,128)}), f32[256,1024]{1,0:T(8,128)}) %all-reduce.7.cloned.1.call-update) | async-done | bytes 1048592 | tf_op jit(solution)/shard_map/psum | solution.py:50
  312.5 0.9 add_convert_fusion.3
  313.4 1.3 collective-permute-start.1
  314.8 1.8 collective-permute-done.1
  316.6 31.3 %all_gather.15 = bf16[256,1024]{1,0:T(8,128)(2,1)S(1)} all-gather(bf16[32,1024]{1,0:T(8,128)(2,1)S(1)} %bitcast_select_fusion), channel_id=1, replica_groups=mesh['section'=4,'tensor'=8] {'tensor'}, dimensions={0}, use_global_device_ids=true | all-gather | bytes 589824 | tf_op jit(solution)/shard_map/all_gather | solution.py:43
  347.9 7.1 %fusion.38 = bf16[256,4096]{1,0:T(8,128)(2,1)S(1)} fusion(bf16[256,1024]{1,0:T(8,128)(2,1)S(1)} %all_gather.15, bf16[1,4096,1024]{2,1,0:T(8,128)(2,1)} %param.13, f32[256,4096]{1,0:T(8,128)} %fusion.26), kind=kOutput, calls=%fused_computation.40 | convolution fusion | flops 2150629376 | bytes 15204352 | tf_op jit(solution)/shard_map/td,fd->tf/dot_general | solution.py:47
  355.0 5.2 %multiply_reduce_fusion = f32[]{:T(128)} fusion(bf16[256,1024]{1,0:T(8,128)(2,1)S(1)} %all_gather.15, bf16[256]{0:T(256)(128)(2,1)S(1)} %get-tuple-element.4, f32[256,4096]{1,0:T(8,128)S(1)} %copy-done.4), kind=kOutput, calls=%fused_computation.2 | convolution fusion | flops 2158231552 | bytes 4719108 | tf_op jit(solution)/shard_map/tf,td->fd/dot_general | solution.py:59
  360.2 5.2 %multiply_reduce_fusion.2 = f32[]{:T(128)} fusion(bf16[256,1024]{1,0:T(8,128)(2,1)S(1)} %all_gather.15, bf16[256]{0:T(256)(128)(2,1)S(1)} %get-tuple-element.3, f32[256,4096]{1,0:T(8,128)S(1)} %copy-done.4), kind=kOutput, calls=%fused_computation.4 | convolution fusion | flops 2158231552 | bytes 4719108 | tf_op jit(solution)/shard_map/tf,td->fd/dot_general | solution.py:59
  365.4 6.5 %multiply_reduce_fusion.1 = f32[]{:T(128)} fusion(bf16[256,4096]{1,0:T(8,128)(2,1)S(1)} %fusion.38, bf16[3,256,1024]{2,1,0:T(8,128)(2,1)} %all-gather.3.cloned.1.call-done, bf16[256]{0:T(256)(128)(2,1)S(1)} %get-tuple-element.4), kind=kOutput, calls=%fused_computation.3 | convolution fusion | flops 2156134400 | bytes 2621956 | tf_op jit(solution)/shard_map/td,tf->df/dot_general | solution.py:56
  373.1 6.3 %multiply_reduce_fusion.3 = f32[]{:T(128)} fusion(bf16[256,4096]{1,0:T(8,128)(2,1)S(1)} %fusion.38, bf16[3,256,1024]{2,1,0:T(8,128)(2,1)} %all-gather.3.cloned.1.call-done, bf16[256]{0:T(256)(128)(2,1)S(1)} %get-tuple-element.3), kind=kOutput, calls=%fused_computation.5 | convolution fusion | flops 2156134400 | bytes 2621956 | tf_op jit(solution)/shard_map/td,tf->df/dot_general | solution.py:56
  380.7 6.7 %fusion.6 = f32[256,1024]{1,0:T(8,128)} fusion(bf16[256,4096]{1,0:T(8,128)(2,1)S(1)} %fusion.38, bf16[1,1024,4096]{2,1,0:T(8,128)(2,1)} %param.12), kind=kOutput, calls=%fused_computation.20 | convolution fusion | flops 2147483648 | bytes 11534336 | tf_op jit(solution)/shard_map/tf,df->td/dot_general | solution.py:49
  387.5 20.4 %all-reduce = (f32[2]{0:T(128)S(1)}, f32[2]{0:T(128)S(1)}, f32[2]{0:T(128)S(1)}) all-reduce(f32[2]{0:T(128)S(1)} %pad_maximum_fusion.1, f32[2]{0:T(128)S(1)} %pad_maximum_fusion.2, f32[2]{0:T(128)S(1)} %pad_maximum_fusion.3), channel_id=1, replica_groups=mesh['section'=4,'tensor'=8] {'tensor'}, use_global_device_ids=true, to_apply=%region_5.6 | all-reduce | flops 6 | bytes 48 | tf_op jit(solution)/shard_map/psum | solution.py:64
  408.2 10.6 %fusion.53 = f32[4096,1024]{1,0:T(8,128)} fusion(bf16[256,1024]{1,0:T(8,128)(2,1)} %copy-done.5, f32[256]{0:T(256)S(1)} %select_reduce_fusion.1, f32[256,4096]{1,0:T(8,128)} %fusion.23), kind=kOutput, calls=%fused_computation.58 | convolution fusion | flops 2150367232 | bytes 21496832 | tf_op jit(solution)/shard_map/tf,td->fd/dot_general | solution.py:72
  418.8 8.2 %fusion.52 = f32[4096,1024]{1,0:T(8,128)} fusion(bf16[1,256,1024]{2,1,0:T(8,128)(2,1)S(1)} %all-gather, f32[256]{0:T(256)S(1)} %select_reduce_fusion.2, f32[256,4096]{1,0:T(8,128)S(1)} %copy-done.1), kind=kOutput, calls=%fused_computation.57 | convolution fusion | flops 2150367232 | bytes 21496832 | tf_op jit(solution)/shard_map/tf,td->fd/dot_general | solution.py:72
  427.0 16.7 %fusion.19 = bf16[1,4096,1024]{2,1,0:T(8,128)(2,1)} fusion(f32[4096,1024]{1,0:T(8,128)} %fusion.52, f32[4096,1024]{1,0:T(8,128)} %fusion.53, bf16[256,1024]{1,0:T(8,128)(2,1)S(1)} %all_gather.15, f32[256]{0:T(256)S(1)} %select_reduce_fusion, f32[256,4096]{1,0:T(8,128)} %fusion.26), kind=kOutput, calls=%fused_computation.33 | convolution fusion | flops 2162950144 | bytes 46662656 | tf_op jit(solution)/shard_map/tf,td->fd/dot_general | solution.py:72
  443.8 10.1 %fusion.47 = f32[1024,4096]{1,0:T(8,128)} fusion(bf16[256,4096]{1,0:T(8,128)(2,1)} %copy-done.6, f32[256]{0:T(256)S(1)} %select_reduce_fusion.2, bf16[3,256,1024]{2,1,0:T(8,128)(2,1)} %all-gather.3.cloned.1.call-done), kind=kOutput, calls=%fused_computation.49 | convolution fusion | flops 2150629376 | bytes 19399680 | tf_op jit(solution)/shard_map/td,tf->df/dot_general | solution.py:69
  453.9 9.3 %fusion.48 = f32[1024,4096]{1,0:T(8,128)} fusion(bf16[256,4096]{1,0:T(8,128)(2,1)S(1)} %copy-done.8, f32[256]{0:T(256)S(1)} %select_reduce_fusion.1, bf16[3,256,1024]{2,1,0:T(8,128)(2,1)} %all-gather.3.cloned.1.call-done), kind=kOutput, calls=%fused_computation.50 | convolution fusion | flops 2150629376 | bytes 19399680 | tf_op jit(solution)/shard_map/td,tf->df/dot_general | solution.py:69
  463.1 16.0 %fusion.18 = bf16[1,1024,4096]{2,1,0:T(8,128)(2,1)} fusion(f32[1024,4096]{1,0:T(8,128)} %fusion.47, f32[1024,4096]{1,0:T(8,128)} %fusion.48, bf16[256,4096]{1,0:T(8,128)(2,1)S(1)} %fusion.38, f32[256]{0:T(256)S(1)} %select_reduce_fusion, bf16[3,256,1024]{2,1,0:T(8,128)(2,1)} %all-gather.3.cloned.1.call-done), kind=kOutput, calls=%fused_computation.32 | convolution fusion | flops 2163212288 | bytes 44565504 | tf_op jit(solution)/shard_map/td,tf->df/dot_general | solution.py:69
  479.2 5.2 %all-reduce.9.cloned.1.call-done = f32[256,1024]{1,0:T(8,128)} async-done(((f32[256,1024]{1,0:T(8,128)}), f32[256,1024]{1,0:T(8,128)}) %all-reduce.9.cloned.1.call-update) | async-done | bytes 1048592 | tf_op jit(solution)/shard_map/psum | solution.py:50
  484.3 0.9 fusion.82
  485.2 0.7 maximum_bitcast_fusion
  (56 shorter events, 1.5 us)
Async XLA Ops:
  7.2 57.0 %all-gather.3.cloned.1.call-start = ((), (), s32[]{:S(2)}) async-start(), calls=%async_computation | async-start | bytes 1769472 | tf_op jit(solution)/shard_map/all_gather | solution.py:36
  16.0 163.1 %all-reduce.5.cloned.1.call-start = ((), (), s32[]{:S(2)}) async-start(), calls=%async_computation.1 | async-start | bytes 2097152 | tf_op jit(solution)/shard_map/psum | solution.py:50
  70.1 10.4 %copy-start = (f32[256,4096]{1,0:T(8,128)}, f32[256,4096]{1,0:T(8,128)S(1)}, u32[]{:S(2)}) copy-start(f32[256,4096]{1,0:T(8,128)S(1)} %fusion.20) | copy-start | bytes 12582916
  70.2 10.4 %slice-start = ((s8[8388608]{0:T(1024)(128)(4,1)}), s8[4194304]{0:T(1024)(128)(4,1)S(1)}, s32[]{:S(2)}) async-start(s8[8388608]{0:T(1024)(128)(4,1)} %bitcast.136), calls=%async_computation.4 | async-start | bytes 8388608
  75.4 5.2 %slice-start.1 = ((s8[8388608]{0:T(1024)(128)(4,1)}), s8[4194304]{0:T(1024)(128)(4,1)S(1)}, s32[]{:S(2)}) async-start(s8[8388608]{0:T(1024)(128)(4,1)} %bitcast.136), calls=%async_computation.5 | async-start | bytes 8388608
  94.2 15.2 %copy-start.6 = (bf16[256,4096]{1,0:T(8,128)(2,1)}, bf16[256,4096]{1,0:T(8,128)(2,1)S(1)}, u32[]{:S(2)}) copy-start(bf16[256,4096]{1,0:T(8,128)(2,1)S(1)} %fusion.44) | copy-start | bytes 6291460
  101.7 210.8 %all-reduce.7.cloned.1.call-start = ((), (), s32[]{:S(2)}) async-start(), calls=%async_computation.2 | async-start | bytes 2097152 | tf_op jit(solution)/shard_map/psum | solution.py:50
  125.0 54.2 %copy-start.9 = (bf16[1,32,1024]{2,1,0:T(8,128)(2,1)S(1)}, bf16[1,32,1024]{2,1,0:T(8,128)(2,1)}, u32[]{:S(2)}) copy-start(bf16[1,32,1024]{2,1,0:T(8,128)(2,1)} %param.10) | copy-start | bytes 196612
  125.0 58.3 %copy-start.10 = (bf16[2,32,1024]{2,1,0:T(8,128)(2,1)S(1)}, bf16[2,32,1024]{2,1,0:T(8,128)(2,1)}, u32[]{:S(2)}) copy-start(bf16[2,32,1024]{2,1,0:T(8,128)(2,1)} %param.11) | copy-start | bytes 393220
  180.1 3.1 collective-permute-start
  214.5 33.5 %copy-start.5 = (bf16[256,1024]{1,0:T(8,128)(2,1)}, bf16[256,1024]{1,0:T(8,128)(2,1)S(1)}, u32[]{:S(2)}) copy-start(bf16[256,1024]{1,0:T(8,128)(2,1)S(1)} %all_gather.14) | copy-start | bytes 1572868
  214.5 7.2 %copy-start.2 = (f32[256,4096]{1,0:T(8,128)S(1)}, f32[256,4096]{1,0:T(8,128)}, u32[]{:S(2)}) copy-start(f32[256,4096]{1,0:T(8,128)} %fusion.23) | copy-start | bytes 12582916
  221.7 19.7 %copy-start.7 = (bf16[256,4096]{1,0:T(8,128)(2,1)}, bf16[256,4096]{1,0:T(8,128)(2,1)S(1)}, u32[]{:S(2)}) copy-start(bf16[256,4096]{1,0:T(8,128)(2,1)S(1)} %fusion.41) | copy-start | bytes 6291460
  233.7 250.6 %all-reduce.9.cloned.1.call-start = ((), (), s32[]{:S(2)}) async-start(), calls=%async_computation.3 | async-start | bytes 2097152 | tf_op jit(solution)/shard_map/psum | solution.py:50
  241.5 6.5 %copy-start.3 = (f32[256,4096]{1,0:T(8,128)S(1)}, f32[256,4096]{1,0:T(8,128)}, u32[]{:S(2)}) copy-start(f32[256,4096]{1,0:T(8,128)} %fusion.23) | copy-start | bytes 12582916
  313.4 3.1 collective-permute-start.1
  347.9 7.1 %copy-start.4 = (f32[256,4096]{1,0:T(8,128)S(1)}, f32[256,4096]{1,0:T(8,128)}, u32[]{:S(2)}) copy-start(f32[256,4096]{1,0:T(8,128)} %fusion.26) | copy-start | bytes 12582916
  408.2 10.6 %copy-start.1 = (f32[256,4096]{1,0:T(8,128)S(1)}, f32[256,4096]{1,0:T(8,128)}, u32[]{:S(2)}) copy-start(f32[256,4096]{1,0:T(8,128)} %copy-done) | copy-start | bytes 12582916
  443.8 10.1 %copy-start.8 = (bf16[256,4096]{1,0:T(8,128)(2,1)S(1)}, bf16[256,4096]{1,0:T(8,128)(2,1)}, u32[]{:S(2)}) copy-start(bf16[256,4096]{1,0:T(8,128)(2,1)} %copy-done.7) | copy-start | bytes 6291460
Sparse Core Ops, SparseCore 0:
  16.2 48.0 all-gather.2
  101.8 77.2 all-reduce.4
  233.8 78.5 all-reduce.6
  408.3 75.9 all-reduce.8
where the time goes:
time: 503 us; the launch traced here: 493 us
  matrix products  212 us (42%)
  waiting for transfers between devices  124 us (25%)
  blocking collectives  117 us (23%)
  between operations  27.8 us (6%)
  other arithmetic  5.36 us (1%)
    psum x3, waiting for transfers between devices, per_device(): summed = lax.psum(own_terms, 'tensor')  108 us
    all_gather x3, blocking collectives, per_device(): grads = lax.all_gather(incoming, 'tensor', axis=0, tiled=True)  96.6 us
    dot_general x6, matrix products, per_device(): jnp.einsum('td,tf->df', inputs * keep, dz, preferred_element_type=jnp.flo...  38.2 us
    dot_general x3, matrix products, per_device(): jnp.einsum('tf,td->fd', hidden, dyc, preferred_element_type=jnp.float32)  35.6 us
    dot_general x3, matrix products, per_device(): jnp.einsum('td,tf->df', inputs, dzc, preferred_element_type=jnp.float32)  35.4 us
    dot_general x6, matrix products, per_device(): jnp.einsum('tf,td->fd', hidden, grads * keep, preferred_element_type=jnp....  31.6 us
    dot_general x3, matrix products, per_device(): jnp.einsum('td,fd->tf', grads, second, preferred_element_type=jnp.float32)  27.9 us
    dot_general x3, matrix products, per_device(): z = jnp.dot(inputs, first, preferred_element_type=jnp.float32)  22.4 us
  transfers between devices with their start and end apart: 6, of which 6 were waited for; matrix products, arithmetic and copies ran while one was open for 24% of the time, Pallas kernels for 0%

commit v1 on v0

--- a/solution.py
+++ b/solution.py
@@ -47,7 +47,11 @@
         back = jnp.einsum("td,fd->tf", grads, second, preferred_element_type=jnp.float32)
         dz = (2.0 * relu * back).astype(jnp.bfloat16)
         own_terms = jnp.einsum("tf,df->td", dz, first, preferred_element_type=jnp.float32)
-        summed = lax.psum(own_terms, "tensor")
+        size = lax.axis_size("tensor")
+        summed, far = (own_terms, 1)
+        while far < size:
+            summed = summed + lax.ppermute(summed, "tensor", [(i, i ^ far) for i in range(size)])
+            far = 2 * far
         shares = lax.dynamic_slice_in_dim(summed, lax.axis_index("tensor") * rows, rows, 0)
         member = membership(example_lengths[0, slot], inputs.shape[0])
         pieces = []

time: 503 us -> 521 us (1.036)
  waiting for transfers between devices: 124 us -> 151 us
  matrix products: 212 us -> 192 us
  starting transfers between devices: 2.93 us -> 9.57 us
  other arithmetic: 5.36 us -> 11.2 us
    ppermute x0 -> x9, waiting for transfers between devices: none -> 135 us  [per_device(): lax.ppermute(summed, 'tensor', [(i, i ^ far) for i in range(size)])]
    psum x3 -> x0, waiting for transfers between devices: 108 us -> none  [per_device(): summed = lax.psum(own_terms, 'tensor')]
    dot_general x3, matrix products: 27.9 us -> 17 us  [per_device(): jnp.einsum('td,fd->tf', grads, second, preferred_element_type=jnp.float32)]
    add x0 -> x6, other arithmetic: none -> 7.58 us  [per_device(): summed + lax.ppermute(summed, 'tensor', [(i, i ^ far) for i in range(size)])]
    ppermute x0 -> x9, starting transfers between devices: none -> 6.68 us  [per_device(): lax.ppermute(summed, 'tensor', [(i, i ^ far) for i in range(size)])]
    dot_general x3, matrix products: 22.4 us -> 16.6 us  [per_device(): z = jnp.dot(inputs, first, preferred_element_type=jnp.float32)]
  transfers between devices with their start and end apart: 6 -> 12, of which waited for: 6 -> 9; matrix products, arithmetic and copies ran while one was open for 24% -> 25% of each run, Pallas kernels for 0% -> 0%
where the time goes in v1:
time: 521 us; the launch traced here: 512 us
  matrix products  192 us (37%)
  waiting for transfers between devices  151 us (29%)
  blocking collectives  117 us (22%)
  between operations  28.4 us (5%)
  other arithmetic  11.2 us (2%)
  starting transfers between devices  9.57 us (2%)
    ppermute x9, waiting for transfers between devices, per_device(): lax.ppermute(summed, 'tensor', [(i, i ^ far) for i in range(size)])  135 us
    all_gather x3, blocking collectives, per_device(): grads = lax.all_gather(incoming, 'tensor', axis=0, tiled=True)  97.1 us
    dot_general x6, matrix products, per_device(): jnp.einsum('td,tf->df', inputs * keep, dz, preferred_element_type=jnp.flo...  37.7 us
    dot_general x3, matrix products, per_device(): jnp.einsum('tf,td->fd', hidden, dyc, preferred_element_type=jnp.float32)  35.4 us
    dot_general x3, matrix products, per_device(): jnp.einsum('td,tf->df', inputs, dzc, preferred_element_type=jnp.float32)  34.3 us
    dot_general x6, matrix products, per_device(): jnp.einsum('tf,td->fd', hidden, grads * keep, preferred_element_type=jnp....  34 us
    psum x1, blocking collectives, per_device(): squares = lax.psum(local_squares, 'tensor')  19.8 us
    dot_general x3, matrix products, per_device(): jnp.einsum('td,fd->tf', grads, second, preferred_element_type=jnp.float32)  17 us
  transfers between devices with their start and end apart: 12, of which 9 were waited for; matrix products, arithmetic and copies ran while one was open for 25% of the time, Pallas kernels for 0%

profile of v1, /device:TPU:0, one launch (start us, length us, event | category | flops | bytes accessed | tf_op | source)
XLA Modules:
  0.0 512.1 jit_solution(15997401446273757355)
XLA Ops:
  7.2 1.4 fusion.88
  16.0 33.8 %all-gather = bf16[1,256,1024]{2,1,0:T(8,128)(2,1)S(1)} all-gather(bf16[1,32,1024]{2,1,0:T(8,128)(2,1)} %param.10), channel_id=2, replica_groups=mesh['section'=4,'tensor'=8] {'tensor'}, dimensions={1}, use_global_device_ids=true | all-gather | bytes 589824 | tf_op jit(solution)/shard_map/all_gather | solution.py:43
  49.8 14.1 %all-gather.3.cloned.1.call-done = bf16[3,256,1024]{2,1,0:T(8,128)(2,1)} async-done(((bf16[3,32,1024]{2,1,0:T(8,128)(2,1)}), bf16[3,256,1024]{2,1,0:T(8,128)(2,1)}) %all-gather.3.cloned.1.call-update) | async-done | bytes 1572880 | tf_op jit(solution)/shard_map/all_gather | solution.py:36
  63.9 6.0 %fusion.20 = f32[256,4096]{1,0:T(8,128)S(1)} fusion(bf16[1,1024,4096]{2,1,0:T(8,128)(2,1)} %param.12, bf16[3,256,1024]{2,1,0:T(8,128)(2,1)} %all-gather.3.cloned.1.call-done), kind=kOutput, calls=%fused_computation.34 | convolution fusion | flops 2148532224 | bytes 13107200 | tf_op jit(solution)/shard_map/dot_general | solution.py:44
  70.0 7.4 %fusion.44 = bf16[256,4096]{1,0:T(8,128)(2,1)S(1)} fusion(bf16[1,4096,1024]{2,1,0:T(8,128)(2,1)} %param.13, f32[256,4096]{1,0:T(8,128)S(1)} %fusion.20, bf16[1,256,1024]{2,1,0:T(8,128)(2,1)S(1)} %all-gather), kind=kOutput, calls=%fused_computation.42 | convolution fusion | flops 2150629376 | bytes 15204352 | tf_op jit(solution)/shard_map/td,fd->tf/dot_general | solution.py:47
  77.4 3.3 fusion.12
  82.3 22.7 %collective-permute-done = f32[256,1024]{1,0:T(8,128)} collective-permute-done((f32[256,1024]{1,0:T(8,128)}, f32[256,1024]{1,0:T(8,128)}, u32[]{:S(2)}, u32[]{:S(2)}) %collective-permute-start) | collective-permute-done | bytes 1048608 | tf_op jit(solution)/shard_map/ppermute | solution.py:53
  105.0 1.7 add.102
  106.7 1.3 collective-permute-start.1
  108.1 7.5 %multiply_reduce_fusion.8 = f32[]{:T(128)} fusion(bf16[1,256,1024]{2,1,0:T(8,128)(2,1)S(1)} %all-gather, bf16[256]{0:T(256)(128)(2,1)S(1)} %get-tuple-element.11, f32[256,4096]{1,0:T(8,128)} %copy-done), kind=kOutput, calls=%fused_computation.10 | convolution fusion | flops 2158231552 | bytes 4719108 | tf_op jit(solution)/shard_map/tf,td->fd/dot_general | solution.py:63
  115.6 14.1 %collective-permute-done.1 = f32[256,1024]{1,0:T(8,128)S(1)} collective-permute-done((f32[256,1024]{1,0:T(8,128)S(1)}, f32[256,1024]{1,0:T(8,128)S(1)}, u32[]{:S(2)}, u32[]{:S(2)}) %collective-permute-start.1) | collective-permute-done | bytes 1048608 | tf_op jit(solution)/shard_map/ppermute | solution.py:53
  129.9 2.4 collective-permute-start.2
  132.3 5.5 %multiply_reduce_fusion.10 = f32[]{:T(128)} fusion(bf16[1,256,1024]{2,1,0:T(8,128)(2,1)S(1)} %all-gather, bf16[256]{0:T(256)(128)(2,1)S(1)} %get-tuple-element.10, f32[256,4096]{1,0:T(8,128)S(1)} %copy-done.1), kind=kOutput, calls=%fused_computation.12 | convolution fusion | flops 2158231552 | bytes 4719108 | tf_op jit(solution)/shard_map/tf,td->fd/dot_general | solution.py:63
  137.9 2.4 fusion.23
  140.3 35.2 %collective-permute-done.2 = f32[256,1024]{1,0:T(8,128)S(1)} collective-permute-done((f32[256,1024]{1,0:T(8,128)S(1)}, f32[256,1024]{1,0:T(8,128)S(1)}, u32[]{:S(2)}, u32[]{:S(2)}) %collective-permute-start.2) | collective-permute-done | bytes 1048608 | tf_op jit(solution)/shard_map/ppermute | solution.py:53
  175.6 1.6 collective-permute-start.3
  177.2 5.3 %multiply_reduce_fusion.9 = f32[]{:T(128)} fusion(bf16[256,4096]{1,0:T(8,128)(2,1)S(1)} %fusion.44, bf16[3,256,1024]{2,1,0:T(8,128)(2,1)S(1)} %copy-done.14, bf16[256]{0:T(256)(128)(2,1)S(1)} %get-tuple-element.11), kind=kOutput, calls=%fused_computation.11 | convolution fusion | flops 2156134400 | bytes 2621956 | tf_op jit(solution)/shard_map/td,tf->df/dot_general | solution.py:60
  182.4 31.9 %all_gather.14 = bf16[256,1024]{1,0:T(8,128)(2,1)S(1)} all-gather(bf16[32,1024]{1,0:T(8,128)(2,1)S(1)} %bitcast_select_fusion.1), channel_id=1, replica_groups=mesh['section'=4,'tensor'=8] {'tensor'}, dimensions={0}, use_global_device_ids=true | all-gather | bytes 589824 | tf_op jit(solution)/shard_map/all_gather | solution.py:43
  214.4 2.5 fusion.41
  216.9 6.5 %fusion.8 = f32[256,1024]{1,0:T(8,128)S(1)} fusion(bf16[256,4096]{1,0:T(8,128)(2,1)S(1)} %fusion.41, bf16[1,1024,4096]{2,1,0:T(8,128)(2,1)} %param.12), kind=kOutput, calls=%fused_computation.22 | convolution fusion | flops 2147483648 | bytes 11534336 | tf_op jit(solution)/shard_map/tf,df->td/dot_general | solution.py:49
  224.6 5.3 %multiply_reduce_fusion.11 = f32[]{:T(128)} fusion(bf16[256,4096]{1,0:T(8,128)(2,1)S(1)} %copy-done.9, bf16[3,256,1024]{2,1,0:T(8,128)(2,1)S(1)} %copy-done.14, bf16[256]{0:T(256)(128)(2,1)S(1)} %get-tuple-element.10), kind=kOutput, calls=%fused_computation.13 | convolution fusion | flops 2156134400 | bytes 2621956 | tf_op jit(solution)/shard_map/td,tf->df/dot_general | solution.py:60
  232.5 8.1 %fusion.26 = f32[256,4096]{1,0:T(8,128)} fusion(bf16[1,1024,4096]{2,1,0:T(8,128)(2,1)} %param.12, bf16[3,256,1024]{2,1,0:T(8,128)(2,1)} %all-gather.3.cloned.1.call-done), kind=kOutput, calls=%fused_computation.36 | convolution fusion | flops 2148532224 | bytes 13107200 | tf_op jit(solution)/shard_map/dot_general | solution.py:44
  240.6 4.0 collective-permute-done.4
  244.5 1.4 add.111
  246.0 6.7 %multiply_reduce_fusion.5 = f32[]{:T(128)} fusion(bf16[256,4096]{1,0:T(8,128)(2,1)S(1)} %copy-done.12, bf16[3,256,1024]{2,1,0:T(8,128)(2,1)} %all-gather.3.cloned.1.call-done, bf16[256]{0:T(256)(128)(2,1)S(1)} %get-tuple-element.9), kind=kOutput, calls=%fused_computation.7 | convolution fusion | flops 2156134400 | bytes 2621956 | tf_op jit(solution)/shard_map/td,tf->df/dot_general | solution.py:60
  252.7 5.3 %multiply_reduce_fusion.4 = f32[]{:T(128)} fusion(bf16[256,1024]{1,0:T(8,128)(2,1)S(1)} %all_gather.14, bf16[256]{0:T(256)(128)(2,1)S(1)} %get-tuple-element.9, f32[256,4096]{1,0:T(8,128)S(1)} %copy-done.4), kind=kOutput, calls=%fused_computation.6 | convolution fusion | flops 2158231552 | bytes 4719108 | tf_op jit(solution)/shard_map/tf,td->fd/dot_general | solution.py:63
  259.3 7.6 %collective-permute-done.5 = f32[256,1024]{1,0:T(8,128)} collective-permute-done((f32[256,1024]{1,0:T(8,128)S(1)}, f32[256,1024]{1,0:T(8,128)}, u32[]{:S(2)}, u32[]{:S(2)}) %collective-permute-start.5) | collective-permute-done | bytes 1048608 | tf_op jit(solution)/shard_map/ppermute | solution.py:53
  266.9 1.4 add.112
  269.2 7.6 %multiply_reduce_fusion.7 = f32[]{:T(128)} fusion(bf16[256,4096]{1,0:T(8,128)(2,1)} %copy-done.11, bf16[3,256,1024]{2,1,0:T(8,128)(2,1)} %all-gather.3.cloned.1.call-done, bf16[256]{0:T(256)(128)(2,1)S(1)} %get-tuple-element.8), kind=kOutput, calls=%fused_computation.9 | convolution fusion | flops 2156134400 | bytes 2621956 | tf_op jit(solution)/shard_map/td,tf->df/dot_general | solution.py:60
  276.9 5.2 %multiply_reduce_fusion.6 = f32[]{:T(128)} fusion(bf16[256,1024]{1,0:T(8,128)(2,1)S(1)} %all_gather.14, bf16[256]{0:T(256)(128)(2,1)S(1)} %get-tuple-element.8, f32[256,4096]{1,0:T(8,128)S(1)} %copy-done.5), kind=kOutput, calls=%fused_computation.8 | convolution fusion | flops 2158231552 | bytes 4719108 | tf_op jit(solution)/shard_map/tf,td->fd/dot_general | solution.py:63
  283.3 26.7 %collective-permute-done.6 = f32[256,1024]{1,0:T(8,128)S(1)} collective-permute-done((f32[256,1024]{1,0:T(8,128)S(1)}, f32[256,1024]{1,0:T(8,128)S(1)}, u32[]{:S(2)}, u32[]{:S(2)}) %collective-permute-start.6) | collective-permute-done | bytes 1048608 | tf_op jit(solution)/shard_map/ppermute | solution.py:53
  311.4 1.8 collective-permute-done.7
  313.2 31.4 %all_gather.15 = bf16[256,1024]{1,0:T(8,128)(2,1)S(1)} all-gather(bf16[32,1024]{1,0:T(8,128)(2,1)S(1)} %bitcast_select_fusion), channel_id=1, replica_groups=mesh['section'=4,'tensor'=8] {'tensor'}, dimensions={0}, use_global_device_ids=true | all-gather | bytes 589824 | tf_op jit(solution)/shard_map/all_gather | solution.py:43
  344.6 7.1 %fusion.38 = bf16[256,4096]{1,0:T(8,128)(2,1)S(1)} fusion(bf16[256,1024]{1,0:T(8,128)(2,1)S(1)} %all_gather.15, bf16[1,4096,1024]{2,1,0:T(8,128)(2,1)} %param.13, f32[256,4096]{1,0:T(8,128)} %fusion.26), kind=kOutput, calls=%fused_computation.40 | convolution fusion | flops 2150629376 | bytes 15204352 | tf_op jit(solution)/shard_map/td,fd->tf/dot_general | solution.py:47
  351.7 5.3 %multiply_reduce_fusion = f32[]{:T(128)} fusion(bf16[256,1024]{1,0:T(8,128)(2,1)S(1)} %all_gather.15, bf16[256]{0:T(256)(128)(2,1)S(1)} %get-tuple-element.4, f32[256,4096]{1,0:T(8,128)S(1)} %copy-done.6), kind=kOutput, calls=%fused_computation.2 | convolution fusion | flops 2158231552 | bytes 4719108 | tf_op jit(solution)/shard_map/tf,td->fd/dot_general | solution.py:63
  357.0 5.2 %multiply_reduce_fusion.2 = f32[]{:T(128)} fusion(bf16[256,1024]{1,0:T(8,128)(2,1)S(1)} %all_gather.15, bf16[256]{0:T(256)(128)(2,1)S(1)} %get-tuple-element.3, f32[256,4096]{1,0:T(8,128)S(1)} %copy-done.6), kind=kOutput, calls=%fused_computation.4 | convolution fusion | flops 2158231552 | bytes 4719108 | tf_op jit(solution)/shard_map/tf,td->fd/dot_general | solution.py:63
  362.2 6.5 %multiply_reduce_fusion.1 = f32[]{:T(128)} fusion(bf16[256,4096]{1,0:T(8,128)(2,1)S(1)} %fusion.38, bf16[3,256,1024]{2,1,0:T(8,128)(2,1)} %all-gather.3.cloned.1.call-done, bf16[256]{0:T(256)(128)(2,1)S(1)} %get-tuple-element.4), kind=kOutput, calls=%fused_computation.3 | convolution fusion | flops 2156134400 | bytes 2621956 | tf_op jit(solution)/shard_map/td,tf->df/dot_general | solution.py:60
  370.0 6.4 %multiply_reduce_fusion.3 = f32[]{:T(128)} fusion(bf16[256,4096]{1,0:T(8,128)(2,1)S(1)} %fusion.38, bf16[3,256,1024]{2,1,0:T(8,128)(2,1)} %all-gather.3.cloned.1.call-done, bf16[256]{0:T(256)(128)(2,1)S(1)} %get-tuple-element.3), kind=kOutput, calls=%fused_computation.5 | convolution fusion | flops 2156134400 | bytes 2621956 | tf_op jit(solution)/shard_map/td,tf->df/dot_general | solution.py:60
  377.7 6.7 %fusion.6 = f32[256,1024]{1,0:T(8,128)} fusion(bf16[256,4096]{1,0:T(8,128)(2,1)S(1)} %fusion.38, bf16[1,1024,4096]{2,1,0:T(8,128)(2,1)} %param.12), kind=kOutput, calls=%fused_computation.20 | convolution fusion | flops 2147483648 | bytes 11534336 | tf_op jit(solution)/shard_map/tf,df->td/dot_general | solution.py:49
  384.5 19.8 %all-reduce = (f32[2]{0:T(128)S(1)}, f32[2]{0:T(128)S(1)}, f32[2]{0:T(128)S(1)}) all-reduce(f32[2]{0:T(128)S(1)} %pad_maximum_fusion.1, f32[2]{0:T(128)S(1)} %pad_maximum_fusion.2, f32[2]{0:T(128)S(1)} %pad_maximum_fusion.3), channel_id=1, replica_groups=mesh['section'=4,'tensor'=8] {'tensor'}, use_global_device_ids=true, to_apply=%region_5.6 | all-reduce | flops 6 | bytes 48 | tf_op jit(solution)/shard_map/psum | solution.py:68
  404.7 10.6 %fusion.53 = f32[4096,1024]{1,0:T(8,128)} fusion(bf16[256,1024]{1,0:T(8,128)(2,1)} %copy-done.7, f32[256]{0:T(256)S(1)} %select_reduce_fusion.1, f32[256,4096]{1,0:T(8,128)} %copy-done.3), kind=kOutput, calls=%fused_computation.58 | convolution fusion | flops 2150367232 | bytes 21496832 | tf_op jit(solution)/shard_map/tf,td->fd/dot_general | solution.py:76
  415.3 8.2 %fusion.52 = f32[4096,1024]{1,0:T(8,128)} fusion(bf16[1,256,1024]{2,1,0:T(8,128)(2,1)S(1)} %all-gather, f32[256]{0:T(256)S(1)} %select_reduce_fusion.2, f32[256,4096]{1,0:T(8,128)S(1)} %copy-done.2), kind=kOutput, calls=%fused_computation.57 | convolution fusion | flops 2150367232 | bytes 21496832 | tf_op jit(solution)/shard_map/tf,td->fd/dot_general | solution.py:76
  423.5 16.6 %fusion.19 = bf16[1,4096,1024]{2,1,0:T(8,128)(2,1)} fusion(f32[4096,1024]{1,0:T(8,128)} %fusion.52, f32[4096,1024]{1,0:T(8,128)} %fusion.53, bf16[256,1024]{1,0:T(8,128)(2,1)S(1)} %all_gather.15, f32[256]{0:T(256)S(1)} %select_reduce_fusion, f32[256,4096]{1,0:T(8,128)} %fusion.26), kind=kOutput, calls=%fused_computation.33 | convolution fusion | flops 2162950144 | bytes 46662656 | tf_op jit(solution)/shard_map/tf,td->fd/dot_general | solution.py:76
  440.1 1.8 add.121
  442.3 9.4 %fusion.47 = f32[1024,4096]{1,0:T(8,128)} fusion(bf16[256,4096]{1,0:T(8,128)(2,1)S(1)} %copy-done.10, f32[256]{0:T(256)S(1)} %select_reduce_fusion.2, bf16[3,256,1024]{2,1,0:T(8,128)(2,1)} %all-gather.3.cloned.1.call-done), kind=kOutput, calls=%fused_computation.49 | convolution fusion | flops 2150629376 | bytes 19399680 | tf_op jit(solution)/shard_map/td,tf->df/dot_general | solution.py:73
  451.8 9.3 %fusion.48 = f32[1024,4096]{1,0:T(8,128)} fusion(bf16[256,4096]{1,0:T(8,128)(2,1)S(1)} %copy-done.13, f32[256]{0:T(256)S(1)} %select_reduce_fusion.1, bf16[3,256,1024]{2,1,0:T(8,128)(2,1)} %all-gather.3.cloned.1.call-done), kind=kOutput, calls=%fused_computation.50 | convolution fusion | flops 2150629376 | bytes 19399680 | tf_op jit(solution)/shard_map/td,tf->df/dot_general | solution.py:73
  462.3 15.6 %fusion.18 = bf16[1,1024,4096]{2,1,0:T(8,128)(2,1)} fusion(f32[1024,4096]{1,0:T(8,128)} %fusion.47, f32[1024,4096]{1,0:T(8,128)} %fusion.48, bf16[256,4096]{1,0:T(8,128)(2,1)S(1)} %fusion.38, f32[256]{0:T(256)S(1)} %select_reduce_fusion, bf16[3,256,1024]{2,1,0:T(8,128)(2,1)} %all-gather.3.cloned.1.call-done), kind=kOutput, calls=%fused_computation.32 | convolution fusion | flops 2163212288 | bytes 44565504 | tf_op jit(solution)/shard_map/td,tf->df/dot_general | solution.py:73
  478.0 25.2 %collective-permute-done.10 = f32[256,1024]{1,0:T(8,128)} collective-permute-done((f32[256,1024]{1,0:T(8,128)}, f32[256,1024]{1,0:T(8,128)}, u32[]{:S(2)}, u32[]{:S(2)}) %collective-permute-start.10) | collective-permute-done | bytes 1048608 | tf_op jit(solution)/shard_map/ppermute | solution.py:53
  (95 shorter events, 10.9 us)
Async XLA Ops:
  7.2 56.7 %all-gather.3.cloned.1.call-start = ((), (), s32[]{:S(2)}) async-start(), calls=%async_computation | async-start | bytes 1769472 | tf_op jit(solution)/shard_map/all_gather | solution.py:36
  63.9 13.5 %slice-start.2 = ((s8[8388608]{0:T(1024)(128)(4,1)}), s8[4194304]{0:T(1024)(128)(4,1)S(1)}, s32[]{:S(2)}) async-start(s8[8388608]{0:T(1024)(128)(4,1)} %bitcast.138), calls=%async_computation.3 | async-start | bytes 8388608
  70.0 7.4 %copy-start = (f32[256,4096]{1,0:T(8,128)}, f32[256,4096]{1,0:T(8,128)S(1)}, u32[]{:S(2)}) copy-start(f32[256,4096]{1,0:T(8,128)S(1)} %fusion.20) | copy-start | bytes 12582916
  70.0 7.4 %slice-start.3 = ((s8[8388608]{0:T(1024)(128)(4,1)}), s8[4194304]{0:T(1024)(128)(4,1)S(1)}, s32[]{:S(2)}) async-start(s8[8388608]{0:T(1024)(128)(4,1)} %bitcast.138), calls=%async_computation.4 | async-start | bytes 8388608
  77.4 99.7 %copy-start.8 = (bf16[256,4096]{1,0:T(8,128)(2,1)}, bf16[256,4096]{1,0:T(8,128)(2,1)S(1)}, u32[]{:S(2)}) copy-start(bf16[256,4096]{1,0:T(8,128)(2,1)S(1)} %fusion.44) | copy-start | bytes 6291460
  77.4 4.0 copy-start.17
  80.8 24.2 %collective-permute-start = (f32[256,1024]{1,0:T(8,128)}, f32[256,1024]{1,0:T(8,128)}, u32[]{:S(2)}, u32[]{:S(2)}) collective-permute-start(f32[256,1024]{1,0:T(8,128)} %fusion.12), channel_id=1, source_target_pairs={{0,1},{1,0},{2,3},{3,2},{4,5},{5,4},{6,7},{7,6},{8,9},{9,8},{10,11... | collective-permute-start | bytes 3145736 | tf_op jit(solution)/shard_map/ppermute | solution.py:53
  106.7 23.1 %collective-permute-start.1 = (f32[256,1024]{1,0:T(8,128)S(1)}, f32[256,1024]{1,0:T(8,128)S(1)}, u32[]{:S(2)}, u32[]{:S(2)}) collective-permute-start(f32[256,1024]{1,0:T(8,128)S(1)} %add.102), channel_id=1, source_target_pairs={{0,2},{1,3},{2,0},{3,1},{4,6},{5,7},{6,4},{7,5},{8,10},{9,11},{10,... | collective-permute-start | bytes 3145736 | tf_op jit(solution)/shard_map/ppermute | solution.py:53
  108.1 24.3 %copy-start.1 = (f32[256,4096]{1,0:T(8,128)S(1)}, f32[256,4096]{1,0:T(8,128)}, u32[]{:S(2)}) copy-start(f32[256,4096]{1,0:T(8,128)} %copy-done) | copy-start | bytes 12582916
  129.8 8.1 %slice-start.4 = ((s8[8388608]{0:T(1024)(128)(4,1)}), s8[4194304]{0:T(1024)(128)(4,1)S(1)}, s32[]{:S(2)}) async-start(s8[8388608]{0:T(1024)(128)(4,1)} %bitcast.140), calls=%async_computation.5 | async-start | bytes 8388608
  129.9 45.6 %collective-permute-start.2 = (f32[256,1024]{1,0:T(8,128)S(1)}, f32[256,1024]{1,0:T(8,128)S(1)}, u32[]{:S(2)}, u32[]{:S(2)}) collective-permute-start(f32[256,1024]{1,0:T(8,128)S(1)} %add.103), channel_id=1, source_target_pairs={{0,4},{1,5},{2,6},{3,7},{4,0},{5,1},{6,2},{7,3},{8,12},{9,13},{10,... | collective-permute-start | bytes 3145736 | tf_op jit(solution)/shard_map/ppermute | solution.py:53
  132.3 5.5 %copy-start.14 = (bf16[3,256,1024]{2,1,0:T(8,128)(2,1)S(1)}, bf16[3,256,1024]{2,1,0:T(8,128)(2,1)}, u32[]{:S(2)}) copy-start(bf16[3,256,1024]{2,1,0:T(8,128)(2,1)} %all-gather.3.cloned.1.call-done) | copy-start | bytes 4718596
  132.3 5.5 %slice-start.5 = ((s8[8388608]{0:T(1024)(128)(4,1)}), s8[4194304]{0:T(1024)(128)(4,1)S(1)}, s32[]{:S(2)}) async-start(s8[8388608]{0:T(1024)(128)(4,1)} %bitcast.140), calls=%async_computation.6 | async-start | bytes 8388608
  137.8 37.7 %copy-start.15 = (bf16[1,32,1024]{2,1,0:T(8,128)(2,1)S(1)}, bf16[1,32,1024]{2,1,0:T(8,128)(2,1)}, u32[]{:S(2)}) copy-start(bf16[1,32,1024]{2,1,0:T(8,128)(2,1)} %param.10) | copy-start | bytes 196612
  140.3 74.0 %copy-start.3 = (f32[256,4096]{1,0:T(8,128)}, f32[256,4096]{1,0:T(8,128)S(1)}, u32[]{:S(2)}) copy-start(f32[256,4096]{1,0:T(8,128)S(1)} %fusion.23) | copy-start | bytes 12582916
  175.5 38.8 %slice-start = ((s8[8388608]{0:T(1024)(128)(4,1)}), s8[4194304]{0:T(1024)(128)(4,1)S(1)}, s32[]{:S(2)}) async-start(s8[8388608]{0:T(1024)(128)(4,1)} %bitcast.136), calls=%async_computation.1 | async-start | bytes 8388608
  175.6 6.9 %copy-start.16 = (bf16[2,32,1024]{2,1,0:T(8,128)(2,1)S(1)}, bf16[2,32,1024]{2,1,0:T(8,128)(2,1)}, u32[]{:S(2)}) copy-start(bf16[2,32,1024]{2,1,0:T(8,128)(2,1)} %param.11) | copy-start | bytes 393220
  175.6 38.8 %slice-start.1 = ((s8[8388608]{0:T(1024)(128)(4,1)}), s8[4194304]{0:T(1024)(128)(4,1)S(1)}, s32[]{:S(2)}) async-start(s8[8388608]{0:T(1024)(128)(4,1)} %bitcast.136), calls=%async_computation.2 | async-start | bytes 8388608
  175.6 6.8 %collective-permute-start.3 = (bf16[32,1024]{1,0:T(8,128)(2,1)S(1)}, bf16[32,1024]{1,0:T(8,128)(2,1)S(1)}, u32[]{:S(2)}, u32[]{:S(2)}) collective-permute-start(bf16[32,1024]{1,0:T(8,128)(2,1)S(1)} %fusion.86), channel_id=1, source_target_pairs={{8,0},{16,8},{24,16},{9,1},{17,9},{25,17},{10,2},{18,10},{26,18},{... | collective-permute-start | bytes 196616 | tf_op jit(solution)/shard_map/ppermute | solution.py:14
  214.4 62.5 %copy-start.7 = (bf16[256,1024]{1,0:T(8,128)(2,1)}, bf16[256,1024]{1,0:T(8,128)(2,1)S(1)}, u32[]{:S(2)}) copy-start(bf16[256,1024]{1,0:T(8,128)(2,1)S(1)} %all_gather.14) | copy-start | bytes 1572868
  216.9 6.6 %copy-start.11 = (bf16[256,4096]{1,0:T(8,128)(2,1)}, bf16[256,4096]{1,0:T(8,128)(2,1)S(1)}, u32[]{:S(2)}) copy-start(bf16[256,4096]{1,0:T(8,128)(2,1)S(1)} %fusion.41) | copy-start | bytes 6291460
  216.9 7.7 %copy-start.9 = (bf16[256,4096]{1,0:T(8,128)(2,1)S(1)}, bf16[256,4096]{1,0:T(8,128)(2,1)}, u32[]{:S(2)}) copy-start(bf16[256,4096]{1,0:T(8,128)(2,1)} %copy-done.8) | copy-start | bytes 6291460
  223.5 21.0 %collective-permute-start.4 = (f32[256,1024]{1,0:T(8,128)S(1)}, f32[256,1024]{1,0:T(8,128)}, u32[]{:S(2)}, u32[]{:S(2)}) collective-permute-start(f32[256,1024]{1,0:T(8,128)S(1)} %fusion.8), channel_id=1, source_target_pairs={{0,1},{1,0},{2,3},{3,2},{4,5},{5,4},{6,7},{7,6},{8,9},{9,8},{10,11... | collective-permute-start | bytes 3145736 | tf_op jit(solution)/shard_map/ppermute | solution.py:53
  232.5 13.5 %copy-start.12 = (bf16[256,4096]{1,0:T(8,128)(2,1)S(1)}, bf16[256,4096]{1,0:T(8,128)(2,1)}, u32[]{:S(2)}) copy-start(bf16[256,4096]{1,0:T(8,128)(2,1)} %copy-done.11) | copy-start | bytes 6291460
  245.9 21.1 %collective-permute-start.5 = (f32[256,1024]{1,0:T(8,128)S(1)}, f32[256,1024]{1,0:T(8,128)}, u32[]{:S(2)}, u32[]{:S(2)}) collective-permute-start(f32[256,1024]{1,0:T(8,128)S(1)} %add.111), channel_id=1, source_target_pairs={{0,2},{1,3},{2,0},{3,1},{4,6},{5,7},{6,4},{7,5},{8,10},{9,11},{10,... | collective-permute-start | bytes 3145736 | tf_op jit(solution)/shard_map/ppermute | solution.py:53
  246.0 6.8 %copy-start.4 = (f32[256,4096]{1,0:T(8,128)S(1)}, f32[256,4096]{1,0:T(8,128)}, u32[]{:S(2)}) copy-start(f32[256,4096]{1,0:T(8,128)} %copy-done.3) | copy-start | bytes 12582916
  268.3 41.7 %collective-permute-start.6 = (f32[256,1024]{1,0:T(8,128)S(1)}, f32[256,1024]{1,0:T(8,128)S(1)}, u32[]{:S(2)}, u32[]{:S(2)}) collective-permute-start(f32[256,1024]{1,0:T(8,128)S(1)} %add.112), channel_id=1, source_target_pairs={{0,4},{1,5},{2,6},{3,7},{4,0},{5,1},{6,2},{7,3},{8,12},{9,13},{10,... | collective-permute-start | bytes 3145736 | tf_op jit(solution)/shard_map/ppermute | solution.py:53
  269.2 7.6 %copy-start.5 = (f32[256,4096]{1,0:T(8,128)S(1)}, f32[256,4096]{1,0:T(8,128)}, u32[]{:S(2)}) copy-start(f32[256,4096]{1,0:T(8,128)} %copy-done.3) | copy-start | bytes 12582916
  310.0 3.1 collective-permute-start.7
  344.6 7.1 %copy-start.6 = (f32[256,4096]{1,0:T(8,128)S(1)}, f32[256,4096]{1,0:T(8,128)}, u32[]{:S(2)}) copy-start(f32[256,4096]{1,0:T(8,128)} %fusion.26) | copy-start | bytes 12582916
  404.6 10.7 %copy-start.2 = (f32[256,4096]{1,0:T(8,128)S(1)}, f32[256,4096]{1,0:T(8,128)}, u32[]{:S(2)}) copy-start(f32[256,4096]{1,0:T(8,128)} %copy-done) | copy-start | bytes 12582916
  404.6 35.5 %collective-permute-start.8 = (f32[256,1024]{1,0:T(8,128)}, f32[256,1024]{1,0:T(8,128)}, u32[]{:S(2)}, u32[]{:S(2)}) collective-permute-start(f32[256,1024]{1,0:T(8,128)} %fusion.6), channel_id=1, source_target_pairs={{0,1},{1,0},{2,3},{3,2},{4,5},{5,4},{6,7},{7,6},{8,9},{9,8},{10,11... | collective-permute-start | bytes 3145736 | tf_op jit(solution)/shard_map/ppermute | solution.py:53
  440.1 2.2 copy-start.10
  442.0 9.8 %copy-start.13 = (bf16[256,4096]{1,0:T(8,128)(2,1)S(1)}, bf16[256,4096]{1,0:T(8,128)(2,1)}, u32[]{:S(2)}) copy-start(bf16[256,4096]{1,0:T(8,128)(2,1)} %copy-done.11) | copy-start | bytes 6291460
  442.0 19.0 %collective-permute-start.9 = (f32[256,1024]{1,0:T(8,128)S(1)}, f32[256,1024]{1,0:T(8,128)S(1)}, u32[]{:S(2)}, u32[]{:S(2)}) collective-permute-start(f32[256,1024]{1,0:T(8,128)S(1)} %add.121), channel_id=1, source_target_pairs={{0,2},{1,3},{2,0},{3,1},{4,6},{5,7},{6,4},{7,5},{8,10},{9,11},{10,... | collective-permute-start | bytes 3145736 | tf_op jit(solution)/shard_map/ppermute | solution.py:53
  462.2 41.0 %collective-permute-start.10 = (f32[256,1024]{1,0:T(8,128)}, f32[256,1024]{1,0:T(8,128)}, u32[]{:S(2)}, u32[]{:S(2)}) collective-permute-start(f32[256,1024]{1,0:T(8,128)} %add.122), channel_id=1, source_target_pairs={{0,4},{1,5},{2,6},{3,7},{4,0},{5,1},{6,2},{7,3},{8,12},{9,13},{10,... | collective-permute-start | bytes 3145736 | tf_op jit(solution)/shard_map/ppermute | solution.py:53
Sparse Core Ops, SparseCore 0:
  16.2 47.6 all-gather.2
